TPU v7x, 32 devices: a whole 2x2x4 slice. The times are simulated.
32 devices in a mesh: orient: 4 (over z), slab: 8 (over y, x, core).
Axes of the slice: x: 2, y: 2, z: 4, core: 2. Of those that a mesh axis runs over, the one named last changes fastest.
Arguments:
- polarization: bfloat16 [8, 2, 3, 8, 9216], P('orient', None, None, 'slab'), may hold values from -6 to 6
- occupied: int32 [8, 9216], P('slab'), may hold values from 0 to 1, as said below
- orient_table: int32 [8, 2], replicated, may hold values from 0 to 15
- dir_index: int32 [2048, 2], replicated, may hold values from 0 to 179
Outputs:
- mueller: float32 [4, 2048], P(None, 'slab')
Inputs may be any that keep to these rules, and one draw needn't show every extreme that they name: 1 marks an occupied dipole cell.
All inputs are finite; a program needn't handle non-finite values.
Results may differ from a plain program's by a relative error of at most 0.00087.
Values may be sent and summed in bfloat16 or wider, within the bound.
A program may use at most 64 MiB of HBM per device.

v0:
```python
import math

import jax
import jax.numpy as jnp
from jax import lax
from jax.sharding import PartitionSpec as P

GX = 96
ORIENT_GRID = 16
THETA_GRID = 180


wave_step = 0.4


def direction_angles(dir_index):
    polar_angle = (dir_index[:, 0].astype(jnp.float32) + 0.5) * (math.pi / THETA_GRID)
    azimuth = dir_index[:, 1].astype(jnp.float32) * (2.0 * math.pi / THETA_GRID)
    return (polar_angle, azimuth)


def unit_vectors(polar_angle, azimuth):
    return (
        jnp.sin(polar_angle) * jnp.cos(azimuth),
        jnp.sin(polar_angle) * jnp.sin(azimuth),
        jnp.cos(polar_angle),
    )


def phase_block(within, plane_index, normals):
    xcoord = (within % GX).astype(jnp.float32)
    ycoord = (within // GX).astype(jnp.float32)
    zcoord = plane_index.astype(jnp.float32)
    angle = wave_step * (
        xcoord[:, None] * normals[0][None, :]
        + ycoord[:, None] * normals[1][None, :]
        + zcoord[:, None] * normals[2][None, :]
    )
    return jnp.concatenate([jnp.cos(angle), -jnp.sin(angle)], axis=1).astype(jnp.bfloat16)


def orient_weights(orient_table):
    turn_angle = orient_table[:, 0].astype(jnp.float32) * (2.0 * math.pi / ORIENT_GRID)
    weight = jnp.sin((orient_table[:, 1].astype(jnp.float32) + 0.5) * (math.pi / ORIENT_GRID))
    return (turn_angle, weight)


def mueller_sum(amplitude, orient_table, polar_angle, azimuth):
    turn_angle, weight = orient_weights(orient_table)
    relative = azimuth[None, :] - turn_angle[:, None]
    cos_polar = jnp.cos(polar_angle)[None, :]
    sin_polar = jnp.sin(polar_angle)[None, :]
    cos_turn = jnp.cos(relative)
    sin_turn = jnp.sin(relative)
    parallel = (cos_polar * cos_turn, cos_polar * sin_turn, -sin_polar)
    across = (-sin_turn, cos_turn, None)

    def project(polar_index, basis_set):
        summed = (
            amplitude[:, polar_index, 0] * basis_set[0][:, None, :]
            + amplitude[:, polar_index, 1] * basis_set[1][:, None, :]
        )
        if basis_set[2] is not None:
            summed = summed + amplitude[:, polar_index, 2] * basis_set[2][:, None, :]
        return summed

    def square(values):
        return values[:, 0] * values[:, 0] + values[:, 1] * values[:, 1]

    lower_right = project(1, across)
    upper_left = project(0, parallel)
    upper_right = project(0, across)
    lower_left = project(1, parallel)
    elem_total = 0.5 * (
        square(lower_right) + square(upper_left) + square(upper_right) + square(lower_left)
    )
    elem_diff = 0.5 * (
        square(upper_left) - square(lower_right) + square(lower_left) - square(upper_right)
    )
    elem_real = (
        lower_right[:, 0] * upper_left[:, 0]
        + lower_right[:, 1] * upper_left[:, 1]
        + upper_right[:, 0] * lower_left[:, 0]
        + upper_right[:, 1] * lower_left[:, 1]
    )
    elem_imag = (
        upper_left[:, 1] * lower_right[:, 0]
        - upper_left[:, 0] * lower_right[:, 1]
        + lower_left[:, 1] * upper_right[:, 0]
        - lower_left[:, 0] * upper_right[:, 1]
    )
    stacked = jnp.stack([elem_total, elem_diff, elem_real, elem_imag])
    return jnp.sum(stacked * weight[None, :, None], axis=1)


def accumulate(flattened, within, plane_index, normals, direction_count):
    cells_here = flattened.shape[1]
    columns = 2 * direction_count
    block_size = math.gcd(cells_here, max(1, (1 << 20) // columns))

    def advance(block_index, summed):
        offset = block_index * block_size
        segment = lax.dynamic_slice_in_dim(flattened, offset, block_size, 1)
        within_block = lax.dynamic_slice_in_dim(within, offset, block_size, 0)
        plane_block = lax.dynamic_slice_in_dim(plane_index, offset, block_size, 0)
        phase = phase_block(within_block, plane_block, normals)
        return summed + jnp.dot(segment, phase, preferred_element_type=jnp.float32)

    initial = jnp.zeros((flattened.shape[0], columns), jnp.float32)
    return lax.fori_loop(0, cells_here // block_size, advance, initial)


def shards(polarization, occupied, orient_table, dir_index):
    local_orients = polarization.shape[0]
    planes = polarization.shape[3]
    plane_cells = polarization.shape[4]
    orient_size = lax.axis_size("orient")
    slab_size = lax.axis_size("slab")
    orient_rank = lax.axis_index("orient")
    slab_rank = lax.axis_index("slab")
    direction_count = dir_index.shape[0]
    polar_angle, azimuth = direction_angles(dir_index)
    masked = polarization * occupied.astype(jnp.bfloat16)[None, None, None]
    grid_cells = planes * plane_cells * slab_size
    weight_total = jnp.sum(orient_weights(orient_table)[1])
    all_orients = local_orients * orient_size
    gathered = lax.all_gather(masked, "orient", axis=0, tiled=True)
    flattened = gathered.reshape(all_orients * 6, planes * plane_cells)
    position = jnp.arange(planes * plane_cells, dtype=jnp.int32)
    within = position % plane_cells
    plane_index = slab_rank * planes + position // plane_cells
    group = direction_count // (slab_size * orient_size)
    own_polar = lax.dynamic_index_in_dim(
        polar_angle.reshape(slab_size, orient_size, group), orient_rank, 1, keepdims=False
    ).reshape(-1)
    own_azimuth = lax.dynamic_index_in_dim(
        azimuth.reshape(slab_size, orient_size, group), orient_rank, 1, keepdims=False
    ).reshape(-1)
    amplitude = accumulate(
        flattened, within, plane_index, unit_vectors(own_polar, own_azimuth), slab_size * group
    )
    amplitude = amplitude.reshape(all_orients * 6, 2, slab_size * group)
    amplitude = lax.psum_scatter(amplitude, "slab", scatter_dimension=2, tiled=True)
    block_polar = lax.dynamic_slice_in_dim(own_polar, slab_rank * group, group, 0)
    block_azimuth = lax.dynamic_slice_in_dim(own_azimuth, slab_rank * group, group, 0)
    summed = mueller_sum(
        amplitude.reshape(all_orients, 2, 3, 2, group), orient_table, block_polar, block_azimuth
    )
    local_result = summed / (weight_total * float(grid_cells))
    return lax.all_gather(local_result, "orient", axis=1, tiled=True)


def solution(mesh):
    return jax.shard_map(
        shards,
        mesh=mesh,
        in_specs=(P("orient", None, None, "slab", None), P("slab", None), P(), P()),
        out_specs=P(None, "slab"),
        check_vma=False,
    )
```

profile of v0, /device:TPU:0, one launch (start us, length us, event | category | flops | bytes accessed | tf_op | source)
XLA Modules:
  0.0 195.2 jit_solution(6054222894584049044)
XLA Ops:
  6.5 0.0 reduce-scatter.4.cloned.1.call-start
  6.5 0.8 multiply_reduce_fusion
  7.4 0.1 mul.543
  7.5 0.1 mul.546
  7.6 0.1 reshape.498
  7.7 0.1 reshape.499
  7.8 0.9 convert_reduce_fusion
  8.7 1.1 broadcast_multiply_fusion
  9.8 22.4 %all_gather.6 = bf16[8,2,3,1,9216]{4,1,3,2,0:T(2,128)(2,1)S(1)} all-gather(bf16[2,2,3,1,9216]{4,1,3,2,0:T(2,128)(2,1)S(1)} %broadcast_multiply_fusion), channel_id=1, replica_groups=mesh['orient'=4,'slab'=8] {'orient'}, dimensions={0}, use_global_device_ids=true | all-gather | bytes 1105920 | tf_op jit(solution)/shard_map/all_gather | solution.py:127
  32.2 0.5 copy.68
  32.7 0.8 reshape.497
  33.6 88.9 %while.16 = (s32[]{:T(128)}, f32[48,1024]{1,0:T(8,128)S(1)}, bf16[48,9216]{1,0:T(8,128)(2,1)S(1)}, s32[9216]{0:T(1024)S(1)}, f32[512]{0:T(512)S(1)}, /*index=5*/...) while((s32[]{:T(128)}, f32[48,1024]{1,0:T(8,128)S(1)}, ...), condition=%wide.region_1.2_spmd.clone, body=%wide.region_0.0_spmd.clone.sunk | while | flops 109689864 | bytes 4724917 | solution.py:110
  33.6 9.3 %cosine_convert_fusion.2 = (bf16[1024,512]{1,0:T(8,128)(2,1)S(1)}, bf16[1024,512]{1,0:T(8,128)(2,1)S(1)}) fusion(f32[512]{0:T(512)S(1)} %get-tuple-element.378, f32[1024]{0:T(1024)S(1)} %get-tuple-element.342, f32[512]{0:T(512)S(1)} %get-tuple-element.376, f32[1024]{0:T(1024)S(1)} %get-tuple-element.343, f32[512]{0:T(512)S(1)} %get-tuple-element.375, ...), kind=kLoop, calls=%fused_computation.5.clone.1 | loop fusion | flops 4718592 | bytes 2115584 | tf_op jit(solution)/shard_map/convert
  42.9 0.5 fusion.37
  43.5 9.3 %cosine_convert_fusion.2 = (bf16[1024,512]{1,0:T(8,128)(2,1)S(1)}, bf16[1024,512]{1,0:T(8,128)(2,1)S(1)}) fusion(f32[512]{0:T(512)S(1)} %get-tuple-element.378, f32[1024]{0:T(1024)S(1)} %get-tuple-element.342, f32[512]{0:T(512)S(1)} %get-tuple-element.376, f32[1024]{0:T(1024)S(1)} %get-tuple-element.343, f32[512]{0:T(512)S(1)} %get-tuple-element.375, ...), kind=kLoop, calls=%fused_computation.5.clone.1 | loop fusion | flops 4718592 | bytes 2115584 | tf_op jit(solution)/shard_map/convert
  52.8 0.5 fusion.37
  53.4 9.3 %cosine_convert_fusion.2 = (bf16[1024,512]{1,0:T(8,128)(2,1)S(1)}, bf16[1024,512]{1,0:T(8,128)(2,1)S(1)}) fusion(f32[512]{0:T(512)S(1)} %get-tuple-element.378, f32[1024]{0:T(1024)S(1)} %get-tuple-element.342, f32[512]{0:T(512)S(1)} %get-tuple-element.376, f32[1024]{0:T(1024)S(1)} %get-tuple-element.343, f32[512]{0:T(512)S(1)} %get-tuple-element.375, ...), kind=kLoop, calls=%fused_computation.5.clone.1 | loop fusion | flops 4718592 | bytes 2115584 | tf_op jit(solution)/shard_map/convert
  62.7 0.5 fusion.37
  63.2 9.3 %cosine_convert_fusion.2 = (bf16[1024,512]{1,0:T(8,128)(2,1)S(1)}, bf16[1024,512]{1,0:T(8,128)(2,1)S(1)}) fusion(f32[512]{0:T(512)S(1)} %get-tuple-element.378, f32[1024]{0:T(1024)S(1)} %get-tuple-element.342, f32[512]{0:T(512)S(1)} %get-tuple-element.376, f32[1024]{0:T(1024)S(1)} %get-tuple-element.343, f32[512]{0:T(512)S(1)} %get-tuple-element.375, ...), kind=kLoop, calls=%fused_computation.5.clone.1 | loop fusion | flops 4718592 | bytes 2115584 | tf_op jit(solution)/shard_map/convert
  72.6 0.5 fusion.37
  73.1 9.3 %cosine_convert_fusion.2 = (bf16[1024,512]{1,0:T(8,128)(2,1)S(1)}, bf16[1024,512]{1,0:T(8,128)(2,1)S(1)}) fusion(f32[512]{0:T(512)S(1)} %get-tuple-element.378, f32[1024]{0:T(1024)S(1)} %get-tuple-element.342, f32[512]{0:T(512)S(1)} %get-tuple-element.376, f32[1024]{0:T(1024)S(1)} %get-tuple-element.343, f32[512]{0:T(512)S(1)} %get-tuple-element.375, ...), kind=kLoop, calls=%fused_computation.5.clone.1 | loop fusion | flops 4718592 | bytes 2115584 | tf_op jit(solution)/shard_map/convert
  82.4 0.5 fusion.37
  83.0 9.3 %cosine_convert_fusion.2 = (bf16[1024,512]{1,0:T(8,128)(2,1)S(1)}, bf16[1024,512]{1,0:T(8,128)(2,1)S(1)}) fusion(f32[512]{0:T(512)S(1)} %get-tuple-element.378, f32[1024]{0:T(1024)S(1)} %get-tuple-element.342, f32[512]{0:T(512)S(1)} %get-tuple-element.376, f32[1024]{0:T(1024)S(1)} %get-tuple-element.343, f32[512]{0:T(512)S(1)} %get-tuple-element.375, ...), kind=kLoop, calls=%fused_computation.5.clone.1 | loop fusion | flops 4718592 | bytes 2115584 | tf_op jit(solution)/shard_map/convert
  92.3 0.5 fusion.37
  92.9 9.3 %cosine_convert_fusion.2 = (bf16[1024,512]{1,0:T(8,128)(2,1)S(1)}, bf16[1024,512]{1,0:T(8,128)(2,1)S(1)}) fusion(f32[512]{0:T(512)S(1)} %get-tuple-element.378, f32[1024]{0:T(1024)S(1)} %get-tuple-element.342, f32[512]{0:T(512)S(1)} %get-tuple-element.376, f32[1024]{0:T(1024)S(1)} %get-tuple-element.343, f32[512]{0:T(512)S(1)} %get-tuple-element.375, ...), kind=kLoop, calls=%fused_computation.5.clone.1 | loop fusion | flops 4718592 | bytes 2115584 | tf_op jit(solution)/shard_map/convert
  102.2 0.5 fusion.37
  102.7 9.3 %cosine_convert_fusion.2 = (bf16[1024,512]{1,0:T(8,128)(2,1)S(1)}, bf16[1024,512]{1,0:T(8,128)(2,1)S(1)}) fusion(f32[512]{0:T(512)S(1)} %get-tuple-element.378, f32[1024]{0:T(1024)S(1)} %get-tuple-element.342, f32[512]{0:T(512)S(1)} %get-tuple-element.376, f32[1024]{0:T(1024)S(1)} %get-tuple-element.343, f32[512]{0:T(512)S(1)} %get-tuple-element.375, ...), kind=kLoop, calls=%fused_computation.5.clone.1 | loop fusion | flops 4718592 | bytes 2115584 | tf_op jit(solution)/shard_map/convert
  112.1 0.5 fusion.37
  112.6 9.3 %cosine_convert_fusion.2 = (bf16[1024,512]{1,0:T(8,128)(2,1)S(1)}, bf16[1024,512]{1,0:T(8,128)(2,1)S(1)}) fusion(f32[512]{0:T(512)S(1)} %get-tuple-element.378, f32[1024]{0:T(1024)S(1)} %get-tuple-element.342, f32[512]{0:T(512)S(1)} %get-tuple-element.376, f32[1024]{0:T(1024)S(1)} %get-tuple-element.343, f32[512]{0:T(512)S(1)} %get-tuple-element.375, ...), kind=kLoop, calls=%fused_computation.5.clone.1 | loop fusion | flops 4718592 | bytes 2115584 | tf_op jit(solution)/shard_map/convert
  122.0 0.5 fusion.37
  122.5 0.2 reshape.500
  122.6 8.5 %copy.76 = f32[48,2,512]{1,0,2:T(8,128)} copy(f32[48,2,512]{2,1,0:T(2,128)S(1)} %reshape.500) | data formatting | bytes 393216
  131.1 0.0 copy-start
  131.1 8.9 %reshape.504 = f32[512,96]{1,0:T(8,128)} reshape(f32[512,48,2]{2,1,0:T(8,128)} %bitcast.74) | data formatting | bytes 393216
  140.1 0.0 reduce-scatter.4.cloned.1.call-update
  140.1 0.1 dynamic_slice.45
  140.2 0.0 copy-done
  140.2 0.6 fusion.26
  141.5 0.1 dynamic-slice_cosine_fusion
  141.6 0.1 broadcast_multiply_fusion.1
  141.7 31.6 %reduce-scatter.4.cloned.1.call-done = f32[64,96]{1,0:T(8,128)} async-done(((f32[512,96]{1,0:T(8,128)}), f32[64,96]{1,0:T(8,128)}) %reduce-scatter.4.cloned.1.call-update) | async-done | bytes 24592
  173.3 1.5 reshape.505
  174.9 0.7 copy.77
  175.6 0.1 fusion.16
  175.7 12.0 %all-gather = f32[4,64,4]{1,2,0:T(4,128)S(1)} all-gather(f32[1,64,4]{1,2,0:T(4,128)S(1)} %divide_bitcast_fusion), channel_id=1, replica_groups=mesh['orient'=4,'slab'=8] {'orient'}, dimensions={0}, use_global_device_ids=true | all-gather | bytes 5120 | tf_op jit(solution)/shard_map/all_gather | solution.py:150
  187.7 0.7 reshape.503
  (21 shorter events, 0.4 us)
Async XLA Ops:
  6.5 166.8 %reduce-scatter.4.cloned.1.call-start = ((), (), s32[]{:S(2)}) async-start(), calls=%async_computation.1 | async-start | bytes 294912
  131.1 9.0 %copy-start = (s32[8,2]{0,1:T(2,128)S(1)}, s32[8,2]{0,1:T(2,128)}, u32[]{:S(2)}) copy-start(s32[8,2]{0,1:T(2,128)} %param.8) | copy-start | bytes 196
Sparse Core Ops, SparseCore 0:
  140.2 33.0 reduce-scatter.3
where the time goes:
time: 196 us; the launch traced here: 195 us
  other arithmetic  88 us (45%)
  blocking collectives  34.4 us (18%)
  waiting for transfers between devices  31.6 us (16%)
  local copies, waits for them, and re-layouts  22.2 us (11%)
  between operations  14.1 us (7%)
  matrix products  4.44 us (2%)
    another operation x9, other arithmetic  83.9 us
    unnamed x2, waiting for transfers between devices  31.6 us
    all_gather x1, blocking collectives, shards(): gathered = lax.all_gather(masked, 'orient', axis=0, tiled=True)  22.4 us
    unnamed x7, local copies, waits for them, and re-layouts  20.3 us
    all_gather x1, blocking collectives, shards(): return lax.all_gather(local_result, 'orient', axis=1, tiled=True)  12 us
    dot_general x9, matrix products, advance(): return summed + jnp.dot(segment, phase, preferred_element_type=jnp.float32)  4.44 us
  transfers between devices with their start and end apart: 1, of which 1 were waited for; matrix products, arithmetic and copies ran while one was open for 0% of the time, Pallas kernels for 0%

commit v1 on v0

v1 whole, which is shorter than its diff:
```python
import functools
import math

import jax
import jax.numpy as jnp
from jax import lax
from jax.experimental import pallas as pl
from jax.experimental.pallas import tpu as pltpu
from jax.sharding import PartitionSpec as P

GX = 96
ORIENT_GRID = 16
THETA_GRID = 180
YL = 8
wave_step = 0.4
MESH = pl.DeviceIdType.MESH
F32 = jnp.float32
BF16 = jnp.bfloat16


def sincos(angle):
    quarter = jnp.round(angle * (2.0 / math.pi))
    rest = angle - quarter * 1.5703125
    rest = rest - quarter * 4.83826794896619e-4
    square = rest * rest
    sine = rest + rest * square * (
        -1.6666654611e-1 + square * (8.3321608736e-3 + square * -1.9515295891e-4)
    )
    cosine = 1.0 - 0.5 * square + square * square * (
        4.166664568298827e-2
        + square * (-1.388731625493765e-3 + square * 2.443315711809948e-5)
    )
    turns = quarter.astype(jnp.int32)
    odd = (turns & 1) == 1
    sin_sign = jnp.where((turns & 2) == 2, -1.0, 1.0)
    cos_sign = jnp.where(((turns + 1) & 2) == 2, -1.0, 1.0)
    return (
        jnp.where(odd, cosine, sine) * sin_sign,
        jnp.where(odd, sine, cosine) * cos_sign,
    )


def flip_index(me, step, size):
    if size & (size - 1):
        return (me + step) % size
    result, bit = 0, 1
    while bit < size:
        result = result + ((me // bit) % 2 + (step // bit) % 2) % 2 * bit
        bit *= 2
    return result


def kernel(
    slab_size, orient_size, planes, cells_all,
    mask_ref, dirs_ref, table_ref, out_ref,
    normal, trig, polar, sent, landed, parts,
    send_sem, recv_sem, part_send, part_recv,
):
    slab = lax.axis_index("slab")
    orient = lax.axis_index("orient")
    rows = mask_ref.shape[1]
    depth = mask_ref.shape[2]
    width = dirs_ref.shape[2]
    group = sent.shape[1] // 2
    pairs = rows // (2 * group)

    barrier = pltpu.get_barrier_semaphore()
    for step in range(1, slab_size):
        pl.semaphore_signal(
            barrier, inc=1, device_id=(orient, flip_index(slab, step, slab_size)),
            device_id_type=MESH,
        )
    for step in range(1, orient_size):
        pl.semaphore_signal(
            barrier, inc=1, device_id=((orient + step) % orient_size, slab),
            device_id_type=MESH,
        )

    dirs = dirs_ref[...].astype(F32)
    sin_p, cos_p = sincos((dirs[:, 0, :] + 0.5) * (math.pi / THETA_GRID))
    sin_a, cos_a = sincos(dirs[:, 1, :] * (2.0 * math.pi / THETA_GRID))
    normal[0] = sin_p * cos_a
    normal[1] = sin_p * sin_a
    normal[2] = cos_p
    polar[0] = sin_p
    polar[1] = cos_p
    polar[2] = sin_a
    polar[3] = cos_a

    line = lax.broadcasted_iota(jnp.int32, (24, 1), 0)
    within = (line % 8).astype(F32)
    coef_x = jnp.where(line < 8, within, jnp.where(line == 16, 8.0, 0.0)) * wave_step
    coef_y = jnp.where(
        (line >= 8) & (line < 16), within,
        jnp.where(line == 17, 2.0 * YL, jnp.where(line == 19, 1.0 * YL, 0.0)),
    ) * wave_step

    def make_tables(index, carry):
        row = pl.ds(index, 1)
        for plane in range(planes):
            depth_at = (slab * planes + plane).astype(F32)
            coef_z = jnp.where((line == 18) | (line == 19), depth_at, 0.0) * wave_step
            angle = (
                coef_x * normal[0, row, :] + coef_y * normal[1, row, :]
                + coef_z * normal[2, row, :]
            )
            sine, cosine = sincos(angle)
            trig[0, plane, index] = cosine
            trig[1, plane, index] = sine
        return carry

    lax.fori_loop(0, slab_size, make_tables, 0)

    def split(values):
        high = values.astype(BF16)
        return high, (values - high.astype(F32)).astype(BF16)

    def chunk(index):
        total = None
        for plane in range(planes):
            cos_t = trig[0, plane, index]
            sin_t = trig[1, plane, index]
            step_c, step_s = cos_t[16:17], sin_t[16:17]
            tile_c, tile_s = cos_t[0:8], sin_t[0:8]
            list_c, list_s = [], []
            for turn in range(GX // 8):
                list_c.append(tile_c)
                list_s.append(tile_s)
                if turn + 1 < GX // 8:
                    tile_c, tile_s = (
                        tile_c * step_c - tile_s * step_s,
                        tile_s * step_c + tile_c * step_s,
                    )
            line_c = jnp.concatenate(list_c, axis=0)
            line_s = jnp.concatenate(list_s, axis=0)
            blocks = [[], [], [], []]
            for y in range(depth // GX):
                y_c, y_s = cos_t[8 + y : 9 + y], sin_t[8 + y : 9 + y]
                c_high, c_low = split(line_c * y_c - line_s * y_s)
                s_high, s_low = split(line_s * y_c + line_c * y_s)
                for held, piece in zip(blocks, (c_high, c_low, s_high, s_low)):
                    held.append(piece)
            c_high, c_low, s_high, s_low = (jnp.concatenate(b, axis=0) for b in blocks)
            masked = mask_ref[plane]
            real = jnp.dot(masked, c_high, preferred_element_type=F32) + jnp.dot(
                masked, c_low, preferred_element_type=F32
            )
            imag = jnp.dot(masked, s_high, preferred_element_type=F32) + jnp.dot(
                masked, s_low, preferred_element_type=F32
            )
            span = 2 * group
            jump_c, jump_s = cos_t[17:18], sin_t[17:18]
            acc_c, acc_s = real[(pairs - 1) * span :], imag[(pairs - 1) * span :]
            for pair in range(pairs - 2, -1, -1):
                part = slice(pair * span, (pair + 1) * span)
                acc_c, acc_s = (
                    acc_c * jump_c - acc_s * jump_s + real[part],
                    acc_s * jump_c + acc_c * jump_s + imag[part],
                )
            lower = lax.broadcasted_iota(jnp.int32, (span, width), 0) < group
            last_c = jnp.where(lower, cos_t[18:19], cos_t[19:20])
            last_s = jnp.where(lower, sin_t[18:19], sin_t[19:20])
            whole_c = acc_c * last_c - acc_s * last_s
            whole_s = acc_s * last_c + acc_c * last_s
            whole_c = whole_c + jnp.concatenate([whole_c[group:], whole_c[:group]], axis=0)
            whole_s = whole_s + jnp.concatenate([whole_s[group:], whole_s[:group]], axis=0)
            here = jnp.where(lower, whole_c, whole_s)
            total = here if total is None else total + here
        return total

    def slab_copy(step):
        peer = flip_index(slab, step, slab_size)
        return pltpu.make_async_remote_copy(
            src_ref=sent.at[step],
            dst_ref=landed.at[step],
            send_sem=send_sem.at[step],
            recv_sem=recv_sem.at[step],
            device_id=(orient, peer),
            device_id_type=MESH,
        )

    pl.semaphore_wait(barrier, slab_size - 1 + orient_size - 1)

    def advance(count, carry):
        step = slab_size - 1 - count
        sent[step] = chunk(flip_index(slab, step, slab_size))
        slab_copy(step).start()
        return carry

    lax.fori_loop(0, slab_size - 1, advance, 0)
    amplitude = chunk(slab)
    for step in range(slab_size - 1, 0, -1):
        slab_copy(step).wait_recv()
        amplitude = amplitude + landed[step]

    weights = sincos((table_ref[...][:, 1:2].astype(F32) + 0.5) * (math.pi / ORIENT_GRID))[0]
    weight_total = jnp.sum(weights, axis=0, keepdims=True)
    local_orients = group // 6
    own = pl.ds(slab, 1)
    sin_p, cos_p = polar[0, own, :], polar[1, own, :]
    sin_a, cos_a = polar[2, own, :], polar[3, own, :]
    own_table = table_ref[pl.ds(orient * local_orients, local_orients), :].astype(F32)
    turn_s, turn_c = sincos(own_table[:, 0:1] * (2.0 * math.pi / ORIENT_GRID))
    own_weight = sincos((own_table[:, 1:2] + 0.5) * (math.pi / ORIENT_GRID))[0]
    results = [0.0, 0.0, 0.0, 0.0]
    for o in range(local_orients):
        t_c, t_s = turn_c[o : o + 1], turn_s[o : o + 1]
        weight = own_weight[o : o + 1]
        cos_q = cos_a * t_c + sin_a * t_s
        sin_q = sin_a * t_c - cos_a * t_s

        def entry(p, c, r):
            at = r * group + o * 6 + p * 3 + c
            return amplitude[at : at + 1]

        def project(p, r):
            first, second, third = entry(p, 0, r), entry(p, 1, r), entry(p, 2, r)
            par = cos_p * (first * cos_q + second * sin_q) - sin_p * third
            across = second * cos_q - first * sin_q
            return par, across

        ul_r, ur_r = project(0, 0)
        ul_i, ur_i = project(0, 1)
        ll_r, lr_r = project(1, 0)
        ll_i, lr_i = project(1, 1)
        lr2 = lr_r * lr_r + lr_i * lr_i
        ul2 = ul_r * ul_r + ul_i * ul_i
        ur2 = ur_r * ur_r + ur_i * ur_i
        ll2 = ll_r * ll_r + ll_i * ll_i
        found = (
            0.5 * (lr2 + ul2 + ur2 + ll2),
            0.5 * (ul2 - lr2 + ll2 - ur2),
            lr_r * ul_r + lr_i * ul_i + ur_r * ll_r + ur_i * ll_i,
            ul_r * lr_i - ul_i * lr_r + ll_r * ur_i - ll_i * ur_r,
        )
        results = [old + weight * new for old, new in zip(results, found)]

    parts[orient] = jnp.concatenate(results, axis=0)

    def part_copy(step):
        return pltpu.make_async_remote_copy(
            src_ref=parts.at[orient],
            dst_ref=parts.at[orient],
            send_sem=part_send.at[step],
            recv_sem=part_recv.at[step],
            device_id=((orient + step) % orient_size, slab),
            device_id_type=MESH,
        )

    for step in range(1, orient_size):
        part_copy(step).start()
    for step in range(slab_size - 1, 0, -1):
        slab_copy(step).wait_send()
    for step in range(1, orient_size):
        back = (orient + orient_size - step) % orient_size
        pltpu.make_async_remote_copy(
            src_ref=parts.at[orient],
            dst_ref=parts.at[back],
            send_sem=part_send.at[step],
            recv_sem=part_recv.at[step],
            device_id=(back, slab),
            device_id_type=MESH,
        ).wait_recv()
    summed = parts[0]
    for o in range(1, orient_size):
        summed = summed + parts[o]
    out_ref[...] = summed / (weight_total * cells_all)
    for step in range(1, orient_size):
        part_copy(step).wait_send()


def shards(slab_size, orient_size, polarization, occupied, orient_table, dir_index):
    orients, _, _, planes, cells = polarization.shape
    group = orients * 6
    depth = YL * GX
    masked = polarization * occupied.astype(BF16)[None, None, None]
    masked = masked.reshape(group, planes, cells // depth, depth)
    masked = masked.transpose(1, 2, 0, 3).reshape(planes, cells // depth * group, depth)
    width = dir_index.shape[0] // slab_size
    dirs = dir_index.T.reshape(2, slab_size, width).transpose(1, 0, 2)
    vmem = pl.BlockSpec(memory_space=pltpu.VMEM)
    return pl.pallas_call(
        functools.partial(
            kernel, slab_size, orient_size, planes, float(planes * slab_size * cells)
        ),
        out_shape=jax.ShapeDtypeStruct((4, width), F32),
        in_specs=[vmem] * 3,
        out_specs=vmem,
        scratch_shapes=[
            pltpu.VMEM((3, slab_size, width), F32),
            pltpu.VMEM((2, planes, slab_size, 24, width), F32),
            pltpu.VMEM((4, slab_size, width), F32),
            pltpu.VMEM((slab_size, 2 * group, width), F32),
            pltpu.VMEM((slab_size, 2 * group, width), F32),
            pltpu.VMEM((orient_size, 4, width), F32),
            pltpu.SemaphoreType.DMA((slab_size,)),
            pltpu.SemaphoreType.DMA((slab_size,)),
            pltpu.SemaphoreType.DMA((orient_size,)),
            pltpu.SemaphoreType.DMA((orient_size,)),
        ],
        compiler_params=pltpu.CompilerParams(collective_id=0, has_side_effects=True),
    )(masked, dirs, orient_table)


def solution(mesh):
    return jax.shard_map(
        functools.partial(shards, mesh.shape["slab"], mesh.shape["orient"]),
        mesh=mesh,
        in_specs=(P("orient", None, None, "slab", None), P("slab", None), P(), P()),
        out_specs=P(None, "slab"),
        check_vma=False,
    )
```

time: 196 us -> 23.2 us (0.12)
  other arithmetic: 88 us -> 2.01 us
  blocking collectives: 34.4 us -> 0 us
  waiting for transfers between devices: 31.6 us -> 0 us
  local copies, waits for them, and re-layouts: 22.2 us -> 3.16 us
  Pallas kernels: 0 us -> 17.7 us
  between operations: 14.1 us -> 0.04 us
  matrix products: 4.44 us -> 0 us
    another operation x9 -> x0, other arithmetic: 83.9 us -> none
    all_gather x2 -> x0, blocking collectives: 34.4 us -> none  [the longest x1 22.4 us: shards(): gathered = lax.all_gather(masked, 'orient', axis=0, tiled=True)]
    unnamed x2 -> x0, waiting for transfers between devices: 31.6 us -> none
    unnamed x7 -> x4, local copies, waits for them, and re-layouts: 20.3 us -> 1.95 us
    pallas_call x0 -> x1, Pallas kernels: none -> 17.7 us  [shards(): pl.pallas_call(functools.partial(kernel, slab_size, orient_size, planes,...]
    dot_general x9 -> x0, matrix products: 4.44 us -> none  [advance(): return summed + jnp.dot(segment, phase, preferred_element_type=jnp.float32)]
  transfers between devices with their start and end apart: 1 -> 0, of which waited for: 1 -> 0; matrix products, arithmetic and copies ran while one was open for 0% -> 0% of each run, Pallas kernels for 0% -> 0%
where the time goes in v1:
time: 23.2 us; the launch traced here: 23 us
  Pallas kernels  17.7 us (76%)
  local copies, waits for them, and re-layouts  3.16 us (14%)
  other arithmetic  2.01 us (9%)
    pallas_call x1, Pallas kernels, shards(): pl.pallas_call(functools.partial(kernel, slab_size, orient_size, planes,...  17.7 us
    unnamed x4, local copies, waits for them, and re-layouts  1.95 us
    mul x1, other arithmetic, shards(): masked = polarization * occupied.astype(BF16)[None, None, None]  1.14 us
    convert_element_type x1, other arithmetic, shards(): masked = polarization * occupied.astype(BF16)[None, None, None]  0.87 us
    reshape x1, local copies, waits for them, and re-layouts, shards(): masked.transpose(1, 2, 0, 3).reshape(planes, cells // depth * group, depth)  0.73 us

profile of v1, /device:TPU:0, one launch (start us, length us, event | category | flops | bytes accessed | tf_op | source)
XLA Modules:
  0.0 23.0 jit_solution(16435476175700290479)
XLA Ops:
  0.0 0.9 %convert_reduce_fusion = bf16[9216]{0:T(1024)(128)(2,1)S(1)} fusion(s32[1,9216]{1,0:T(1,128)} %param.5), kind=kLoop, calls=%fused_computation.1 | loop fusion | flops 9216 | bytes 55296 | tf_op jit(solution)/shard_map/convert_element_type | solution.py:276
  0.9 1.1 %broadcast_multiply_fusion = bf16[2,2,3,1,9216]{4,1,3,2,0:T(2,128)(2,1)S(1)} fusion(bf16[2,2,3,1,9216]{4,1,3,2,0:T(2,128)(2,1)} %param.4, bf16[9216]{0:T(1024)(128)(2,1)S(1)} %convert_reduce_fusion), kind=kLoop, calls=%fused_computation | loop fusion | flops 110592 | bytes 460800 | tf_op jit(solution)/shard_map/mul | solution.py:276
  2.0 0.1 copy.6
  2.1 0.3 %reshape.12 = bf16[12,1,12,768]{3,2,0,1:T(8,128)(2,1)S(1)} reshape(bf16[2,2,3,1,9216]{4,2,1,0,3:T(4,128)(2,1)S(1)} %copy.6) | data formatting | bytes 442368 | tf_op jit(solution)/shard_map/reshape | solution.py:277
  2.4 0.1 copy.7
  2.5 0.0 copy-start
  2.5 0.7 %reshape.13.mask_ref = bf16[1,144,768]{2,1,0:T(8,128)(2,1)} reshape(bf16[1,12,12,768]{3,2,1,0:T(8,128)(2,1)S(1)} %copy.7) | data formatting | bytes 442368 | tf_op jit(solution)/shard_map/reshape | solution.py:278
  3.3 0.0 copy-done
  3.3 0.7 %copy.8.table_ref = s32[8,2]{1,0:T(8,128)} copy(s32[8,2]{0,1:T(2,128)S(1)} %copy-done) | data formatting | bytes 128 | tf_op args[2]
  3.9 17.7 %shard_map.46 = f32[4,256]{1,0:T(4,128)} custom-call(bf16[1,144,768]{2,1,0:T(8,128)(2,1)} %reshape.13.mask_ref, s32[8,2,256]{2,1,0:T(2,128)} %bitcast.9, s32[8,2]{1,0:T(8,128)} %copy.8.table_ref), custom_call_target="tpu_custom_call" | custom-call | tf_op jit(solution)/shard_map/pallas_call | solution.py:282
  21.7 1.3 %copy.10 = f32[4,256]{1,0:T(4,128)} copy(f32[4,256]{1,0:T(4,128)} %shard_map.46) | data formatting | bytes 8192
Async XLA Ops:
  2.5 0.7 %copy-start = (s32[8,2]{0,1:T(2,128)S(1)}, s32[8,2]{0,1:T(2,128)}, u32[]{:S(2)}) copy-start(s32[8,2]{0,1:T(2,128)} %param.6) | copy-start | bytes 196

commit v2 on v1

v2 whole, which is shorter than its diff:
```python
import functools
import math

import jax
import jax.numpy as jnp
from jax import lax
from jax.experimental import pallas as pl
from jax.experimental.pallas import tpu as pltpu
from jax.sharding import PartitionSpec as P

GX = 96
ORIENT_GRID = 16
THETA_GRID = 180
YL = 4
MB = 4
wave_step = 0.4
MESH = pl.DeviceIdType.MESH
F32 = jnp.float32
BF16 = jnp.bfloat16


def sincos(angle):
    quarter = jnp.round(angle * (2.0 / math.pi))
    rest = angle - quarter * 1.5703125
    rest = rest - quarter * 4.83826794896619e-4
    square = rest * rest
    sine = rest + rest * square * (
        -1.6666654611e-1 + square * (8.3321608736e-3 + square * -1.9515295891e-4)
    )
    cosine = 1.0 - 0.5 * square + square * square * (
        4.166664568298827e-2
        + square * (-1.388731625493765e-3 + square * 2.443315711809948e-5)
    )
    turns = quarter.astype(jnp.int32)
    odd = (turns & 1) == 1
    sin_sign = jnp.where((turns & 2) == 2, -1.0, 1.0)
    cos_sign = jnp.where(((turns + 1) & 2) == 2, -1.0, 1.0)
    return (
        jnp.where(odd, cosine, sine) * sin_sign,
        jnp.where(odd, sine, cosine) * cos_sign,
    )


def flip_index(me, step, size):
    if size & (size - 1):
        return (me + step) % size
    result, bit = 0, 1
    while bit < size:
        result = result + ((me // bit) % 2 + (step // bit) % 2) % 2 * bit
        bit *= 2
    return result


def kernel(
    slab_size, orient_size, cells_all,
    table_ref, dirs_ref, pol_ref, occ_ref, out_ref,
    normal, trig, basis, held_pol, held_occ, mask, phases, sent, landed, parts,
    load_sem, send_sem, recv_sem, part_send, part_recv,
):
    slab = lax.axis_index("slab")
    orient = lax.axis_index("orient")
    loads = [
        pltpu.make_async_copy(pol_ref, held_pol, load_sem.at[0]),
        pltpu.make_async_copy(occ_ref, held_occ, load_sem.at[1]),
    ]
    for load in loads:
        load.start()
    local_orients, components, planes, _, cells = pol_ref.shape
    all_orients = table_ref.shape[1]
    width = dirs_ref.shape[2]
    group = sent.shape[1] // 2
    span = 2 * group
    depth = YL * GX
    pairs = cells // depth // 2

    barrier = pltpu.get_barrier_semaphore()
    for step in range(1, slab_size):
        pl.semaphore_signal(
            barrier, inc=1, device_id=(orient, flip_index(slab, step, slab_size)),
            device_id_type=MESH,
        )
    for step in range(1, orient_size):
        pl.semaphore_signal(
            barrier, inc=1, device_id=((orient + step) % orient_size, slab),
            device_id_type=MESH,
        )

    dirs = dirs_ref[...].astype(F32)
    azimuth = dirs[:, 1, :] * (2.0 * math.pi / THETA_GRID)
    sin_p, cos_p = sincos((dirs[:, 0, :] + 0.5) * (math.pi / THETA_GRID))
    sin_a, cos_a = sincos(azimuth)
    normal[0] = sin_p * cos_a
    normal[1] = sin_p * sin_a
    normal[2] = cos_p
    normal[3] = sin_p
    normal[4] = azimuth

    line = lax.broadcasted_iota(jnp.int32, (24, 1), 0)
    middle = 0.5 * (YL - 1)
    coef_x = jnp.where(
        line < 8, line.astype(F32), jnp.where(line == 16, 8.0, 0.0)
    ) * wave_step
    coef_y = jnp.where(
        (line >= 8) & (line < 16), line.astype(F32) - 7.5,
        jnp.where(
            line == 17, 2.0 * YL,
            jnp.where(line == 18, middle, jnp.where(line == 19, YL + middle, 0.0)),
        ),
    ) * wave_step

    together = math.gcd(slab_size, 4)

    def make_tables(block, carry):
        for inner in range(together):
            index = block * together + inner
            row = pl.ds(index, 1)
            for plane in range(planes):
                depth_at = (slab * planes + plane).astype(F32)
                coef_z = jnp.where((line == 18) | (line == 19), depth_at, 0.0) * wave_step
                angle = (
                    coef_x * normal[0, row, :] + coef_y * normal[1, row, :]
                    + coef_z * normal[2, row, :]
                )
                sine, cosine = sincos(angle)
                trig[0, plane, index] = cosine
                trig[1, plane, index] = sine
        return carry

    lax.fori_loop(0, slab_size // together, make_tables, 0)

    tilt_row = lax.broadcasted_iota(jnp.int32, (all_orients, width), 0)
    tilts = jnp.zeros((all_orients, width), F32)
    for o in range(all_orients):
        tilts = jnp.where(tilt_row == o, table_ref[1, o].astype(F32), tilts)
    weights = sincos((tilts + 0.5) * (math.pi / ORIENT_GRID))[0]
    share = 1.0 / (jnp.sum(weights, axis=0, keepdims=True) * cells_all)
    own = pl.ds(slab, 1)
    for o in range(local_orients):
        turn = table_ref[0, orient * local_orients + o].astype(F32)
        tilt = table_ref[1, orient * local_orients + o].astype(F32)
        turns = jnp.full((1, width), turn, F32) * (2.0 * math.pi / ORIENT_GRID)
        sin_q, cos_q = sincos(normal[4, own, :] - turns)
        scaled = (jnp.full((1, width), tilt, F32) + 0.5) * (math.pi / ORIENT_GRID)
        basis[o, 0:1] = sin_q
        basis[o, 1:2] = cos_q
        basis[o, 2:3] = sincos(scaled)[0] * share

    for load in loads:
        load.wait()

    def place(block, carry):
        for plane in range(planes):
            for part in range(MB):
                at = pl.ds(pl.multiple_of((block * MB + part) * depth, 128), depth)
                kept = held_occ[pl.ds(plane, 1), at].astype(F32).astype(BF16)
                for o in range(local_orients):
                    for c in range(components):
                        piece = held_pol[o, c, plane, :, at] * kept
                        first = part * group + (o * components + c) * 2
                        mask[plane, block, first : first + 2, 0:depth] = piece
                        mask[plane, block, first : first + 2, depth : 2 * depth] = piece
        return carry

    lax.fori_loop(0, cells // depth // MB, place, 0)

    def generate(index, plane, slot):
        cos_t = trig[0, plane, index]
        sin_t = trig[1, plane, index]
        step_c, step_s = cos_t[16:17], sin_t[16:17]
        tile_c, tile_s = cos_t[0:8], sin_t[0:8]

        def put(kind, first, values):
            high = values.astype(BF16)
            phases[slot, kind, first : first + 16] = high
            phases[slot, kind, depth + first : depth + first + 16] = (
                values - high.astype(F32)
            ).astype(BF16)

        for turn in range(GX // 16):
            next_c = tile_c * step_c - tile_s * step_s
            next_s = tile_s * step_c + tile_c * step_s
            line_c = jnp.concatenate([tile_c, next_c], axis=0)
            line_s = jnp.concatenate([tile_s, next_s], axis=0)
            for y in range(YL // 2):
                y_c, y_s = cos_t[8 + y : 9 + y], sin_t[8 + y : 9 + y]
                cc, ss = line_c * y_c, line_s * y_s
                sc, cs = line_s * y_c, line_c * y_s
                above = (YL // 2 + y) * GX + turn * 16
                below = (YL // 2 - 1 - y) * GX + turn * 16
                put(0, above, cc - ss)
                put(0, below, cc + ss)
                put(1, above, sc + cs)
                put(1, below, sc - cs)
            if turn + 1 < GX // 16:
                tile_c = next_c * step_c - next_s * step_s
                tile_s = next_s * step_c + next_c * step_s

    def multiply(index, plane, slot):
        masked = mask[plane].reshape(pairs * span, 2 * depth)
        real = jnp.dot(masked, phases[slot, 0], preferred_element_type=F32)
        imag = jnp.dot(masked, phases[slot, 1], preferred_element_type=F32)
        cos_t = trig[0, plane, index]
        sin_t = trig[1, plane, index]
        jump_c, jump_s = cos_t[17:18], sin_t[17:18]
        acc_c, acc_s = real[(pairs - 1) * span :], imag[(pairs - 1) * span :]
        for pair in range(pairs - 2, -1, -1):
            part = slice(pair * span, (pair + 1) * span)
            acc_c, acc_s = (
                acc_c * jump_c - acc_s * jump_s + real[part],
                acc_s * jump_c + acc_c * jump_s + imag[part],
            )
        lower = lax.broadcasted_iota(jnp.int32, (span, width), 0) < group
        last_c = jnp.where(lower, cos_t[18:19], cos_t[19:20])
        last_s = jnp.where(lower, sin_t[18:19], sin_t[19:20])
        whole_c = acc_c * last_c - acc_s * last_s
        whole_s = acc_s * last_c + acc_c * last_s
        whole_c = whole_c + jnp.concatenate([whole_c[group:], whole_c[:group]], axis=0)
        whole_s = whole_s + jnp.concatenate([whole_s[group:], whole_s[:group]], axis=0)
        return jnp.where(lower, whole_c, whole_s)

    def slab_copy(step):
        peer = flip_index(slab, step, slab_size)
        return pltpu.make_async_remote_copy(
            src_ref=sent.at[step],
            dst_ref=landed.at[step],
            send_sem=send_sem.at[step],
            recv_sem=recv_sem.at[step],
            device_id=(orient, peer),
            device_id_type=MESH,
        )

    def target(count):
        return flip_index(slab, slab_size - 1 - count, slab_size)

    def stage(count, slot, last):
        index = target(count)
        step = slab_size - 1 - count
        total = None
        for plane in range(planes):
            now = (slot + plane) % 2
            if plane + 1 < planes:
                generate(index, plane + 1, 1 - now)
            elif not last:
                generate(target(count + 1), 0, 1 - now)
            here = multiply(index, plane, now)
            total = here if total is None else total + here
        sent[step] = total
        if not last:
            slab_copy(step).start()

    def advance(turn, carry):
        stage(2 * turn, 0, False)
        stage(2 * turn + 1, planes % 2, False)
        return carry

    generate(target(0), 0, 0)
    pl.semaphore_wait(barrier, slab_size - 1 + orient_size - 1)
    lax.fori_loop(0, slab_size // 2 - 1, advance, 0)
    stage(slab_size - 2, 0, False)
    stage(slab_size - 1, planes % 2, True)

    amplitude = sent[0]
    for step in range(slab_size - 1, 0, -1):
        slab_copy(step).wait_recv()
        amplitude = amplitude + landed[step]

    sin_p, cos_p = normal[3, own, :], normal[2, own, :]
    results = [0.0, 0.0, 0.0, 0.0]
    for o in range(local_orients):
        sin_q, cos_q, weight = basis[o, 0:1], basis[o, 1:2], basis[o, 2:3]

        def entry(p, c, r):
            at = r * group + (o * 3 + c) * 2 + p
            return amplitude[at : at + 1]

        def project(p, r):
            first, second, third = entry(p, 0, r), entry(p, 1, r), entry(p, 2, r)
            par = cos_p * (first * cos_q + second * sin_q) - sin_p * third
            across = second * cos_q - first * sin_q
            return par, across

        ul_r, ur_r = project(0, 0)
        ul_i, ur_i = project(0, 1)
        ll_r, lr_r = project(1, 0)
        ll_i, lr_i = project(1, 1)
        lr2 = lr_r * lr_r + lr_i * lr_i
        ul2 = ul_r * ul_r + ul_i * ul_i
        ur2 = ur_r * ur_r + ur_i * ur_i
        ll2 = ll_r * ll_r + ll_i * ll_i
        found = (
            0.5 * (lr2 + ul2 + ur2 + ll2),
            0.5 * (ul2 - lr2 + ll2 - ur2),
            lr_r * ul_r + lr_i * ul_i + ur_r * ll_r + ur_i * ll_i,
            ul_r * lr_i - ul_i * lr_r + ll_r * ur_i - ll_i * ur_r,
        )
        results = [old + weight * new for old, new in zip(results, found)]

    parts[orient] = jnp.concatenate(results, axis=0)

    def part_copy(step):
        return pltpu.make_async_remote_copy(
            src_ref=parts.at[orient],
            dst_ref=parts.at[orient],
            send_sem=part_send.at[step],
            recv_sem=part_recv.at[step],
            device_id=((orient + step) % orient_size, slab),
            device_id_type=MESH,
        )

    for step in range(1, orient_size):
        part_copy(step).start()
    for step in range(slab_size - 1, 0, -1):
        slab_copy(step).wait_send()
    for step in range(1, orient_size):
        back = (orient + orient_size - step) % orient_size
        pltpu.make_async_remote_copy(
            src_ref=parts.at[orient],
            dst_ref=parts.at[back],
            send_sem=part_send.at[step],
            recv_sem=part_recv.at[step],
            device_id=(back, slab),
            device_id_type=MESH,
        ).wait_recv()
    summed = parts[0]
    for o in range(1, orient_size):
        summed = summed + parts[o]
    out_ref[...] = summed
    for step in range(1, orient_size):
        part_copy(step).wait_send()


def shards(slab_size, orient_size, polarization, occupied, orient_table, dir_index):
    orients, _, components, planes, cells = polarization.shape
    group = orients * 6
    depth = YL * GX
    pol = polarization.transpose(0, 2, 3, 1, 4)
    width = dir_index.shape[0] // slab_size
    dirs = dir_index.T.reshape(2, slab_size, width).transpose(1, 0, 2)
    vmem = pl.BlockSpec(memory_space=pltpu.VMEM)
    anywhere = pl.BlockSpec(memory_space=pltpu.HBM)
    return pl.pallas_call(
        functools.partial(
            kernel, slab_size, orient_size, float(planes * slab_size * cells)
        ),
        out_shape=jax.ShapeDtypeStruct((4, width), F32),
        in_specs=[pl.BlockSpec(memory_space=pltpu.SMEM), vmem, anywhere, anywhere],
        out_specs=vmem,
        scratch_shapes=[
            pltpu.VMEM((5, slab_size, width), F32),
            pltpu.VMEM((2, planes, slab_size, 24, width), F32),
            pltpu.VMEM((orients, 3, width), F32),
            pltpu.VMEM(pol.shape, BF16),
            pltpu.VMEM(occupied.shape, jnp.int32),
            pltpu.VMEM((planes, cells // depth // MB, MB * group, 2 * depth), BF16),
            pltpu.VMEM((2, 2, 2 * depth, width), BF16),
            pltpu.VMEM((slab_size, 2 * group, width), F32),
            pltpu.VMEM((slab_size, 2 * group, width), F32),
            pltpu.VMEM((orient_size, 4, width), F32),
            pltpu.SemaphoreType.DMA((2,)),
            pltpu.SemaphoreType.DMA((slab_size,)),
            pltpu.SemaphoreType.DMA((slab_size,)),
            pltpu.SemaphoreType.DMA((orient_size,)),
            pltpu.SemaphoreType.DMA((orient_size,)),
        ],
        compiler_params=pltpu.CompilerParams(
            collective_id=0, has_side_effects=True
        ),
    )(orient_table.T, dirs, pol, occupied)


def solution(mesh):
    return jax.shard_map(
        functools.partial(shards, mesh.shape["slab"], mesh.shape["orient"]),
        mesh=mesh,
        in_specs=(P("orient", None, None, "slab", None), P("slab", None), P(), P()),
        out_specs=P(None, "slab"),
        check_vma=False,
    )
```

time: 23.2 us -> 18.1 us (0.78)
  other arithmetic: 2.01 us -> 0 us
  local copies, waits for them, and re-layouts: 3.16 us -> 1.28 us
  Pallas kernels: 17.7 us -> 16.5 us
    pallas_call x1, Pallas kernels: 17.7 us -> 16.5 us  [shards(): pl.pallas_call(functools.partial(kernel, slab_size, orient_size, float(pl...]
    mul x1 -> x0, other arithmetic: 1.14 us -> none  [shards(): masked = polarization * occupied.astype(BF16)[None, None, None]]
    reshape x2 -> x0, local copies, waits for them, and re-layouts: 1.03 us -> none  [the longest x1 0.73 us: shards(): masked.transpose(1, 2, 0, 3).reshape(planes, cells // depth * group, depth)]
    convert_element_type x1 -> x0, other arithmetic: 0.87 us -> none  [shards(): masked = polarization * occupied.astype(BF16)[None, None, None]]
    unnamed x4 -> x1, local copies, waits for them, and re-layouts: 1.95 us -> 1.28 us
where the time goes in v2:
time: 18.1 us; the launch traced here: 17.8 us
  Pallas kernels  16.5 us (91%)
  local copies, waits for them, and re-layouts  1.28 us (7%)
    pallas_call x1, Pallas kernels, shards(): pl.pallas_call(functools.partial(kernel, slab_size, orient_size, float(pl...  16.5 us
    unnamed x1, local copies, waits for them, and re-layouts  1.28 us

profile of v2, /device:TPU:0, one launch (start us, length us, event | category | flops | bytes accessed | tf_op | source)
XLA Modules:
  0.0 17.8 jit_solution(16053561383803433402)
XLA Ops:
  0.0 16.5 %shard_map.46 = f32[4,256]{1,0:T(4,128)} custom-call(s32[2,8]{1,0:T(2,128)} %bitcast.9, s32[8,2,256]{2,1,0:T(2,128)} %bitcast.8, bf16[2,3,1,2,9216]{4,3,2,1,0:T(2,128)(2,1)} %bitcast.7, s32[1,9216]{1,0:T(1,128)} %occ_ref.1), custom_call_target="tpu_custom_call" | custom-call | tf_op jit(solution)/shard_map/pallas_call | solution.py:341
  16.5 1.3 %copy.6 = f32[4,256]{1,0:T(4,128)} copy(f32[4,256]{1,0:T(4,128)} %shard_map.46) | data formatting | bytes 8192

commit v3 on v2

--- a/solution.py
+++ b/solution.py
@@ -53,13 +53,15 @@
 
 def kernel(
     slab_size, orient_size, cells_all,
-    table_ref, dirs_ref, pol_ref, occ_ref, out_ref,
-    normal, trig, basis, held_pol, held_occ, mask, phases, sent, landed, parts,
+    table_hbm, dirs_hbm, pol_ref, occ_ref, out_ref,
+    table_ref, dirs_ref, normal, trig, basis, held_pol, held_occ, mask, phases, sent, landed, parts,
     load_sem, send_sem, recv_sem, part_send, part_recv,
 ):
     slab = lax.axis_index("slab")
     orient = lax.axis_index("orient")
     loads = [
+        pltpu.make_async_copy(dirs_hbm, dirs_ref, load_sem.at[2]),
+        pltpu.make_async_copy(table_hbm, table_ref, load_sem.at[3]),
         pltpu.make_async_copy(pol_ref, held_pol, load_sem.at[0]),
         pltpu.make_async_copy(occ_ref, held_occ, load_sem.at[1]),
     ]
@@ -85,6 +87,7 @@
             device_id_type=MESH,
         )
 
+    loads[0].wait()
     dirs = dirs_ref[...].astype(F32)
     azimuth = dirs[:, 1, :] * (2.0 * math.pi / THETA_GRID)
     sin_p, cos_p = sincos((dirs[:, 0, :] + 0.5) * (math.pi / THETA_GRID))
@@ -128,6 +131,7 @@
 
     lax.fori_loop(0, slab_size // together, make_tables, 0)
 
+    loads[1].wait()
     tilt_row = lax.broadcasted_iota(jnp.int32, (all_orients, width), 0)
     tilts = jnp.zeros((all_orients, width), F32)
     for o in range(all_orients):
@@ -145,7 +149,7 @@
         basis[o, 1:2] = cos_q
         basis[o, 2:3] = sincos(scaled)[0] * share
 
-    for load in loads:
+    for load in loads[2:]:
         load.wait()
 
     def place(block, carry):
@@ -153,12 +157,13 @@
             for part in range(MB):
                 at = pl.ds(pl.multiple_of((block * MB + part) * depth, 128), depth)
                 kept = held_occ[pl.ds(plane, 1), at].astype(F32).astype(BF16)
-                for o in range(local_orients):
-                    for c in range(components):
-                        piece = held_pol[o, c, plane, :, at] * kept
-                        first = part * group + (o * components + c) * 2
-                        mask[plane, block, first : first + 2, 0:depth] = piece
-                        mask[plane, block, first : first + 2, depth : 2 * depth] = piece
+                pieces = [
+                    held_pol[o, c, plane, :, at]
+                    for o in range(local_orients)
+                    for c in range(components)
+                ]
+                rows = jnp.concatenate(pieces, axis=0) * kept
+                mask[plane, block, part * group : (part + 1) * group, :] = rows
         return carry
 
     lax.fori_loop(0, cells // depth // MB, place, 0)
@@ -196,7 +201,8 @@
                 tile_s = next_s * step_c + next_c * step_s
 
     def multiply(index, plane, slot):
-        masked = mask[plane].reshape(pairs * span, 2 * depth)
+        masked = mask[plane].reshape(pairs * span, depth)
+        masked = jnp.concatenate([masked, masked], axis=1)
         real = jnp.dot(masked, phases[slot, 0], preferred_element_type=F32)
         imag = jnp.dot(masked, phases[slot, 1], preferred_element_type=F32)
         cos_t = trig[0, plane, index]
@@ -342,21 +348,23 @@
         functools.partial(
             kernel, slab_size, orient_size, float(planes * slab_size * cells)
         ),
-        out_shape=jax.ShapeDtypeStruct((4, width), F32),
-        in_specs=[pl.BlockSpec(memory_space=pltpu.SMEM), vmem, anywhere, anywhere],
+        out_shape=pltpu.VMEM((4, width), F32),
+        in_specs=[anywhere] * 4,
         out_specs=vmem,
         scratch_shapes=[
+            pltpu.SMEM((2, orient_table.shape[0]), jnp.int32),
+            pltpu.VMEM(dirs.shape, jnp.int32),
             pltpu.VMEM((5, slab_size, width), F32),
             pltpu.VMEM((2, planes, slab_size, 24, width), F32),
             pltpu.VMEM((orients, 3, width), F32),
             pltpu.VMEM(pol.shape, BF16),
             pltpu.VMEM(occupied.shape, jnp.int32),
-            pltpu.VMEM((planes, cells // depth // MB, MB * group, 2 * depth), BF16),
+            pltpu.VMEM((planes, cells // depth // MB, MB * group, depth), BF16),
             pltpu.VMEM((2, 2, 2 * depth, width), BF16),
             pltpu.VMEM((slab_size, 2 * group, width), F32),
             pltpu.VMEM((slab_size, 2 * group, width), F32),
             pltpu.VMEM((orient_size, 4, width), F32),
-            pltpu.SemaphoreType.DMA((2,)),
+            pltpu.SemaphoreType.DMA((4,)),
             pltpu.SemaphoreType.DMA((slab_size,)),
             pltpu.SemaphoreType.DMA((slab_size,)),
             pltpu.SemaphoreType.DMA((orient_size,)),

time: 18.1 us -> 16.1 us (0.89)
  Pallas kernels: 16.5 us -> 15.3 us
  local copies, waits for them, and re-layouts: 1.28 us -> 0.6 us
    pallas_call x1, Pallas kernels: 16.5 us -> 15.3 us  [shards(): pl.pallas_call(functools.partial(kernel, slab_size, orient_size, float(pl...]
    unnamed x1, local copies, waits for them, and re-layouts: 1.28 us -> 0.6 us
where the time goes in v3:
time: 16.1 us; the launch traced here: 15.9 us
  Pallas kernels  15.3 us (95%)
  local copies, waits for them, and re-layouts  0.6 us (4%)
    pallas_call x1, Pallas kernels, shards(): pl.pallas_call(functools.partial(kernel, slab_size, orient_size, float(pl...  15.3 us
    unnamed x1, local copies, waits for them, and re-layouts  0.6 us

profile of v3, /device:TPU:0, one launch (start us, length us, event | category | flops | bytes accessed | tf_op | source)
XLA Modules:
  0.0 15.9 jit_solution(11049052317267886995)
XLA Ops:
  0.0 15.3 %shard_map.46 = f32[4,256]{1,0:T(4,128)S(1)} custom-call(s32[2,8]{1,0:T(2,128)} %bitcast.9, s32[8,2,256]{2,1,0:T(2,128)} %bitcast.8, bf16[2,3,1,2,9216]{4,3,2,1,0:T(2,128)(2,1)} %bitcast.7, s32[1,9216]{1,0:T(1,128)} %occ_ref.1), custom_call_target="tpu_custom_call" | custom-call | tf_op jit(solution)/shard_map/pallas_call | solution.py:347
  15.3 0.6 %copy.6 = f32[4,256]{1,0:T(4,128)} copy(f32[4,256]{1,0:T(4,128)S(1)} %shard_map.46) | data formatting | bytes 8192
